TPU v7x, 32 devices: a whole 2x2x4 slice. The times are simulated.
32 devices in a mesh: groups: 1, row: 32 (over z, y, x, core).
Axes of the slice: x: 2, y: 2, z: 4, core: 2. Of those that a mesh axis runs over, the one named last changes fastest.
Arguments:
- sub_vectors: float32 [8192, 2, 8192], P('groups', None, 'row'), may hold values from -6 to 6
- eigen_values: float32 [2, 8192], P(None, ('groups', 'row')), may hold values from -16384 to 16384, as said below
- kept: int32 [2, 8192], P(None, ('groups', 'row')), may hold values from 0 to 1, as said below
- poles: int32 [2, 128], P(None, 'groups'), may hold values from 0 to 16383, as said below
- coupling: float32 [1], P('groups'), may hold values from 0.5 to 2
Outputs:
- position: float32 [128], P('groups')
- merged: float32 [8192, 2, 128], P(('groups', 'row'))
Inputs may be any that keep to these rules, and one draw needn't show every extreme that they name: `kept`: exactly 4096 entries are 0. All named entries are kept; poles[0, k] and poles[1, k] are neighbours among the kept eigenvalues in increasing order, poles[1, k] the larger; with S = 96, the rank of poles[0, k] among the kept eigenvalues (rank 0 the smallest) lies between k * S and (k + 1) * S - 2. `eigen_values`: all distinct; neighbouring values in sorted order differ by 0.25 or more.
All inputs are finite; a program needn't handle non-finite values.
Results may differ from a plain program's by a relative error of at most 0.0003.
Values sent between devices are 32-bit elements; how exact they have to be, the bound alone decides.
A program may use at most 128 MiB of HBM per device.

v0:
```python
import jax
import jax.numpy as jnp
from jax import lax
from jax.sharding import PartitionSpec as P

ITERS = 5


def secular_terms(weights, shifted, offset):
    inverse = 1.0 / (shifted - offset[:, None])
    part = weights[None, :] * inverse
    return (jnp.sum(part, 1), jnp.sum(part * inverse, 1))


def newton_update(offset, total, slope, coupling, spacing):
    moved = offset - (1.0 / coupling[0] + total) / slope
    return jnp.clip(moved, 0.02 * spacing, 0.98 * spacing)


def body(sub_vectors, eigen_values, kept, poles, coupling):
    row_count = sub_vectors.shape[0]
    row_devices = lax.axis_size("row")
    kept_float = kept.astype(jnp.float32)
    boundary = jnp.stack([sub_vectors[row_count - 1, 0, :], sub_vectors[0, 1, :]])
    masked_z = boundary * kept_float
    masked_d = eigen_values - 1000000.0 * (1.0 - kept_float)
    full_z, full_d = (
        lax.all_gather(masked_z, "row", axis=1, tiled=True),
        lax.all_gather(masked_d, "row", axis=1, tiled=True),
    )
    pole_values = full_d.reshape(-1)[poles]
    root_total = poles.shape[1]
    lower = pole_values[0]
    spacing = pole_values[1] - lower
    portion = root_total // row_devices
    first_root = lax.axis_index("row") * portion
    own_lower = lax.dynamic_slice_in_dim(lower, first_root, portion, 0)
    own_spacing = lax.dynamic_slice_in_dim(spacing, first_root, portion, 0)
    weights = (full_z * full_z).reshape(-1)
    shifted = full_d.reshape(-1)[None, :] - own_lower[:, None]
    own_offset = 0.5 * own_spacing
    for step in range(ITERS):
        total, slope = secular_terms(weights, shifted, own_offset)
        own_offset = newton_update(own_offset, total, slope, coupling, own_spacing)
    unused, own_sq = secular_terms(weights, shifted, own_offset)
    offset, norm_sq = (
        lax.all_gather(own_offset, "row", axis=0, tiled=True),
        lax.all_gather(own_sq, "row", axis=0, tiled=True),
    )
    position = offset / spacing
    normalizer = 1.0 / jnp.sqrt(norm_sq)
    vectors = masked_z[:, :, None] / (masked_d[:, :, None] - lower - offset) * normalizer
    merged = lax.psum_scatter(
        jnp.einsum("isj,sjk->isk", sub_vectors, vectors, precision=lax.Precision.HIGHEST),
        "row",
        scatter_dimension=0,
        tiled=True,
    )
    return (position, merged)


def solution(mesh):
    in_specs = (
        P("groups", None, "row"),
        P(None, ("groups", "row")),
        P(None, ("groups", "row")),
        P(None, "groups"),
        P("groups"),
    )
    out_specs = (P("groups"), P(("groups", "row"), None, None))
    return jax.shard_map(body, mesh=mesh, in_specs=in_specs, out_specs=out_specs, check_vma=False)
```

profile of v0, /device:TPU:0, one launch (start us, length us, event | category | flops | bytes accessed | tf_op | source)
XLA Modules:
  0.0 316.5 jit_solution(12328028618224150138)
XLA Ops:
  7.2 0.0 reduce-scatter.2.cloned.1.call-start
  7.9 0.7 fusion.26
  8.5 0.7 slice_bitcast_fusion.1
  9.3 0.7 maximum_multiply_fusion
  10.0 43.4 %all_gather.13 = f32[2,8192]{1,0:T(2,128)S(1)} all-gather(f32[2,256]{1,0:T(2,128)S(1)} %get-tuple-element.26), channel_id=1, replica_groups=mesh['groups'=1,'row'=32] {'row'}, dimensions={1}, use_global_device_ids=true | all-gather | bytes 67584 | tf_op jit(solution)/shard_map/all_gather | solution.py:28
  53.4 36.8 %all_gather.12 = f32[2,8192]{1,0:T(2,128)S(1)} all-gather(f32[2,256]{1,0:T(2,128)S(1)} %get-tuple-element.27), channel_id=1, replica_groups=mesh['groups'=1,'row'=32] {'row'}, dimensions={1}, use_global_device_ids=true | all-gather | bytes 67584 | tf_op jit(solution)/shard_map/all_gather | solution.py:29
  90.2 1.7 gather_fusion
  92.0 0.1 dynamic-slice.1
  92.1 0.1 broadcast_multiply_fusion
  92.2 0.4 multiply_reduce_fusion.4
  92.6 0.4 multiply_reduce_fusion.3
  93.0 0.4 multiply_reduce_fusion.2
  93.5 0.4 multiply_reduce_fusion.1
  93.9 0.4 multiply_reduce_fusion
  94.3 0.1 fusion.27
  94.4 0.3 fusion.10
  94.8 0.2 dynamic-update-slice.1
  95.0 37.1 %all-reduce.2 = (f32[128]{0:T(128)S(1)}, f32[128]{0:T(128)S(1)}) all-reduce(f32[128]{0:T(128)S(1)} %get-tuple-element.20, f32[128]{0:T(128)S(1)} %dynamic-update-slice.1), channel_id=1, replica_groups=mesh['groups'=1,'row'=32] {'row'}, use_global_device_ids=true, to_apply=%add | all-reduce | flops 256 | bytes 2048
  132.1 24.1 %fusion.2 = f32[8192,2,128]{0,2,1:T(8,128)} fusion(f32[8192,2,256]{2,1,0:T(2,128)} %param.5, f32[128]{0:T(128)S(1)} %sqrt.3, f32[128]{0:T(128)S(1)} %get-tuple-element.18, f32[128]{0:T(128)S(1)} %get-tuple-element.28, f32[2,256]{1,0:T(2,128)S(1)} %get-tuple-element.27, f32[2,256]{1,0:T(2,128)S(1)} %get-tuple-element.26), kind=kOutput, calls=%fused_computation.3 | convolution fusion | flops 6442713088 | bytes 25171456 | tf_op jit(solution)/shard_map/isj,sjk->isk/dot_general | solution.py:54
  156.1 0.0 reduce-scatter.2.cloned.1.call-update
  156.2 0.5 div.68
  156.7 151.2 %reduce-scatter.2.cloned.1.call-done = f32[256,2,128]{0,2,1:T(8,128)} async-done(((f32[8192,2,128]{0,2,1:T(8,128)}), f32[256,2,128]{0,2,1:T(8,128)}) %reduce-scatter.2.cloned.1.call-update) | async-done | bytes 262160 | tf_op jit(solution)/shard_map/reduce_scatter | solution.py:53
  307.9 1.8 copy.12
  (12 shorter events, 0.1 us)
Async XLA Ops:
  7.2 300.7 %reduce-scatter.2.cloned.1.call-start = ((), (), s32[]{:S(2)}) async-start(), calls=%async_computation.1 | async-start | bytes 8650752 | tf_op jit(solution)/shard_map/reduce_scatter | solution.py:53
Sparse Core Ops, SparseCore 0:
  156.3 151.5 reduce-scatter.1
where the time goes:
time: 317 us; the launch traced here: 316 us
  waiting for transfers between devices  151 us (48%)
  blocking collectives  117 us (37%)
  matrix products  24.1 us (8%)
  between operations  14.8 us (5%)
  other arithmetic  4.56 us (1%)
  local copies, waits for them, and re-layouts  4.54 us (1%)
    reduce_scatter x1, waiting for transfers between devices, body(): lax.psum_scatter(jnp.einsum('isj,sjk->isk', sub_vectors, vectors, precisi...  151 us
    all_gather x1, blocking collectives, body(): lax.all_gather(masked_z, 'row', axis=1, tiled=True)  43.4 us
    unnamed x1, blocking collectives  37.1 us
    all_gather x1, blocking collectives, body(): lax.all_gather(masked_d, 'row', axis=1, tiled=True)  36.8 us
    dot_general x1, matrix products, body(): jnp.einsum('isj,sjk->isk', sub_vectors, vectors, precision=lax.Precision....  24.1 us
  transfers between devices with their start and end apart: 1, of which 1 were waited for; matrix products, arithmetic and copies ran while one was open for 0% of the time, Pallas kernels for 0%

commit v1 on v0

v1 whole, which is shorter than its diff:
```python
import functools

import jax
import jax.numpy as jnp
from jax import lax
from jax.experimental import pallas as pl
from jax.experimental.pallas import tpu as pltpu
from jax.sharding import PartitionSpec as P

ITERS = 5
MESH = pl.DeviceIdType.MESH
LANES = 128


def total_of(x):
    return jnp.sum(jnp.sum(x, axis=0, keepdims=True), axis=1, keepdims=True)


def kernel(
    n,
    inner_chips,
    packed,
    portion,
    poles,
    coupling,
    payload,
    index,
    z_column,
    d_column,
    sub,
    position,
    merged,
    gathered,
    full_z,
    full_d,
    own_roots,
    roots,
    held,
    factors,
    partial,
    partner_partial,
    mine,
    arrived,
    reduced_a,
    reduced_b,
    last_a,
    last_b,
    load_sem,
    gather_send,
    gather_recv,
    roots_send,
    roots_recv,
    pair_send,
    pair_recv,
    first_send,
    first_recv,
    a_send,
    a_recv,
    b_send,
    b_recv,
):
    me = lax.axis_index("row")
    chips = n // 2
    core = lax.rem(me, 2)
    chip = me // 2
    size_a = inner_chips
    size_b = chips // size_a
    place_a = lax.rem(chip, size_a)
    place_b = chip // size_a
    rows, root_total = partial.shape[2], partial.shape[3]
    tile_rows = sub.shape[0] // (rows * n)
    blocks = tile_rows // 2
    columns = blocks * LANES
    loads = load_sem.shape[0]
    load_rows = sub.shape[0] // loads

    def load(i):
        part = pl.ds(pl.multiple_of(i * load_rows, 8), load_rows)
        return pltpu.make_async_copy(sub.at[part], held.at[part], load_sem.at[i])

    for i in range(loads):
        load(i).start()

    barrier = pltpu.get_barrier_semaphore()

    def greet(i, carry):
        pl.semaphore_signal(barrier, inc=1, device_id={"row": lax.rem(me + i, n)}, device_id_type=MESH)
        return carry

    lax.fori_loop(1, n, greet, 0)
    pl.semaphore_wait(barrier, n - 1)

    def push(source, target, send, recv):
        def step(i, carry):
            pltpu.make_async_remote_copy(
                src_ref=source,
                dst_ref=target.at[i - 1],
                send_sem=send,
                recv_sem=recv,
                device_id={"row": lax.rem(me + i, n)},
                device_id_type=MESH,
            ).start()
            return carry

        lax.fori_loop(1, n, step, 0)

    def settle(target, sem):
        whole = target.at[pl.ds(0, n - 1)]
        pltpu.make_async_copy(whole, whole, sem).wait()

    push(payload, gathered, gather_send, gather_recv)
    settle(gathered, gather_recv)
    half = payload.shape[0] // 2
    full_z[pl.ds(0, packed), :] = payload[pl.ds(0, packed), :]
    full_d[pl.ds(0, packed), :] = payload[pl.ds(half, packed), :]
    for i in range(1, n):
        full_z[pl.ds(i * packed, packed), :] = gathered[i - 1, pl.ds(0, packed), :]
        full_d[pl.ds(i * packed, packed), :] = gathered[i - 1, pl.ds(half, packed), :]
    values = full_d[...]
    weights = full_z[...] * full_z[...]
    slot = index[0]
    within = index[1]
    owner = lax.rem(me - slot + n, n)
    places = within + owner * columns
    inverse_coupling = 1.0 / coupling[0]
    lane = lax.broadcasted_iota(jnp.int32, (1, root_total), 1)
    rows_out = [jnp.zeros((1, root_total), jnp.float32) for _ in range(4)]
    for r in range(portion):
        k = me * portion + r
        lower = total_of(jnp.where(places == poles[0, k], values, 0.0))
        spacing = total_of(jnp.where(places == poles[1, k], values, 0.0)) - lower
        shifted = values - lower
        offset = 0.5 * spacing
        for step in range(ITERS + 1):
            inverse = 1.0 / (shifted - offset)
            part = weights * inverse
            slope = total_of(part * inverse)
            if step < ITERS:
                moved = offset - (inverse_coupling + total_of(part)) / slope
                offset = jnp.minimum(jnp.maximum(moved, 0.02 * spacing), 0.98 * spacing)
        for i, value in enumerate((lower, spacing, offset, slope)):
            rows_out[i] = jnp.where(lane == k, value, rows_out[i])
    for i in range(4):
        own_roots[pl.ds(i, 1), :] = rows_out[i]
    own_roots[pl.ds(4, 4), :] = jnp.zeros((4, root_total), jnp.float32)
    push(own_roots, roots, roots_send, roots_recv)
    settle(roots, roots_recv)
    known = own_roots[...]
    for i in range(n - 1):
        known = known + roots[i]
    lower, spacing, offset, norm_sq = (known[i : i + 1, :] for i in range(4))
    position[...] = offset / spacing
    vectors = z_column[...] / ((d_column[...] - lower) - offset) * (1.0 / jnp.sqrt(norm_sq))
    top = vectors.astype(jnp.bfloat16)
    factors[:, pl.ds(0, root_total)] = top
    factors[:, pl.ds(root_total, root_total)] = (vectors - top.astype(jnp.float32)).astype(jnp.bfloat16)

    for i in range(loads):
        load(i).wait()

    outer = (size_b, size_a)
    inner = (size_a, size_b)

    def target_chip(s, u, v):
        step_a, step_b = (v, u) if s == 0 else (u, v)
        new_a = lax.rem(place_a + step_a + 1, size_a)
        new_b = lax.rem(place_b + step_b + 1, size_b)
        return new_a, new_b

    def product(s, device):
        start = device * (rows * tile_rows)
        pieces = [held[pl.ds(start + j * 2 + s, rows, stride=tile_rows), :] for j in range(blocks)]
        a = pieces[0] if blocks == 1 else jnp.concatenate(pieces, axis=1)
        high = a.astype(jnp.bfloat16)
        low = (a - high.astype(jnp.float32)).astype(jnp.bfloat16)
        right = factors[pl.ds(s * columns, columns), :]
        both = jnp.dot(high, right, preferred_element_type=jnp.float32)
        small = jnp.dot(low, right[:, :root_total], preferred_element_type=jnp.float32)
        return both[:, :root_total] + (both[:, root_total:] + small)

    def pair_copy(s, t):
        return pltpu.make_async_remote_copy(
            src_ref=partial.at[s, t],
            dst_ref=partner_partial.at[s, t],
            send_sem=pair_send.at[s, t],
            recv_sem=pair_recv.at[s, t],
            device_id={"row": chip * 2 + 1 - core},
            device_id_type=MESH,
        )

    def first_copy(s, t):
        u, v = t // inner[s], lax.rem(t, inner[s])
        new_a, new_b = target_chip(s, u, v)
        peer = place_b * size_a + new_a if s == 0 else new_b * size_a + place_a
        return pltpu.make_async_remote_copy(
            src_ref=mine.at[s, t],
            dst_ref=arrived.at[s, t],
            send_sem=first_send.at[s, t],
            recv_sem=first_recv.at[s, t],
            device_id={"row": peer * 2 + core},
            device_id_type=MESH,
        )

    def device_of(s, t, which):
        new_a, new_b = target_chip(s, t // inner[s], lax.rem(t, inner[s]))
        return (new_b * size_a + new_a) * 2 + which

    def for_partner(t, carry):
        for s in range(2):
            partial[s, t] = product(s, device_of(s, t, 1 - core))
            pair_copy(s, t).start()
        return carry

    lax.fori_loop(0, chips, for_partner, 0)

    def for_self(t, carry):
        for s in range(2):
            value = product(s, device_of(s, t, core))
            pair_copy(s, t).wait_recv()
            mine[s, t] = value + partner_partial[s, t]

            @pl.when(lax.rem(t, inner[s]) != inner[s] - 1)
            def _():
                first_copy(s, t).start()

        return carry

    lax.fori_loop(0, chips, for_self, 0)

    reduced, last = (reduced_a, reduced_b), (last_a, last_b)
    sends, recvs = (a_send, b_send), (a_recv, b_recv)

    def second_copy(s, u):
        new_a, new_b = target_chip(s, u, u)
        peer = new_b * size_a + place_a if s == 0 else place_b * size_a + new_a
        return pltpu.make_async_remote_copy(
            src_ref=reduced[s].at[u],
            dst_ref=last[s].at[u],
            send_sem=sends[s].at[u],
            recv_sem=recvs[s].at[u],
            device_id={"row": peer * 2 + core},
            device_id_type=MESH,
        )

    def fold(s, u):
        base = u * inner[s]
        value = mine[s, base + inner[s] - 1]
        for v in range(inner[s] - 1):
            first_copy(s, base + v).wait_recv()
            value = value + arrived[s, base + v]
        reduced[s][u] = value

    for u in range(max(outer)):
        for s in range(2):
            if u < outer[s]:
                fold(s, u)
                if u < outer[s] - 1:
                    second_copy(s, u).start()

    for s in range(2):
        value = reduced[s][outer[s] - 1]
        for u in range(outer[s] - 1):
            second_copy(s, u).wait_recv()
            value = value + last[s][u]
        strips = root_total // LANES
        for strip in range(strips):
            merged[pl.ds(strip * 2 + s, rows, stride=2 * strips), :] = value[:, strip * LANES : (strip + 1) * LANES]

    settle(gathered, gather_send)
    settle(roots, roots_send)

    def drain(t, carry):
        for s in range(2):
            pair_copy(s, t).wait_send()

            @pl.when(lax.rem(t, inner[s]) != inner[s] - 1)
            def _():
                first_copy(s, t).wait_send()

        return carry

    lax.fori_loop(0, chips, drain, 0)
    for s in range(2):
        for u in range(outer[s] - 1):
            second_copy(s, u).wait_send()


def body(sub_vectors, eigen_values, kept, poles, coupling):
    order, _, columns = sub_vectors.shape
    n = lax.axis_size("row")
    root_total = poles.shape[1]
    portion = root_total // n
    strips = root_total // LANES
    rows = order // n
    chips = n // 2
    inner_chips = 4 if chips % 4 == 0 else 1
    outer_chips = chips // inner_chips
    blocks = columns // LANES
    packed = 2 * blocks
    half = -(-packed // 4) * 4

    kept_float = kept.astype(jnp.float32)
    boundary = jnp.stack([sub_vectors[order - 1, 0, :], sub_vectors[0, 1, :]])
    masked_z = boundary * kept_float
    masked_d = eigen_values - 1000000.0 * (1.0 - kept_float)
    tall = lambda x: jnp.pad(x.reshape(packed, LANES), ((0, half - packed), (0, 0)))
    payload = jnp.concatenate([tall(masked_z), tall(masked_d)], axis=0)
    slot = jnp.broadcast_to(jnp.arange(n, dtype=jnp.int32)[:, None, None], (n, packed, LANES))
    within = (
        jnp.arange(2, dtype=jnp.int32)[:, None] * order + jnp.arange(columns, dtype=jnp.int32)[None, :]
    ).reshape(1, packed, LANES)
    within = jnp.broadcast_to(within, (n, packed, LANES))
    index = jnp.stack([slot, within]).reshape(2, n * packed, LANES)
    view = (
        sub_vectors.reshape(order, 2, blocks, LANES)
        .transpose(0, 2, 1, 3)
        .reshape(order * blocks * 2, LANES)
    )
    vmem = pl.BlockSpec(memory_space=pltpu.VMEM)
    smem = pl.BlockSpec(memory_space=pltpu.SMEM)
    chunk = (rows, root_total)
    f32 = jnp.float32
    dma = pltpu.SemaphoreType.DMA
    position, merged = pl.pallas_call(
        functools.partial(kernel, n, inner_chips, packed, portion),
        out_shape=(
            jax.ShapeDtypeStruct((1, root_total), f32),
            jax.ShapeDtypeStruct((rows * 2 * strips, LANES), f32),
        ),
        in_specs=[smem, smem, vmem, vmem, vmem, vmem, pl.BlockSpec(memory_space=pl.ANY)],
        out_specs=(vmem, vmem),
        scratch_shapes=[
            pltpu.VMEM((n - 1, 2 * half, LANES), f32),
            pltpu.VMEM((n * packed, LANES), f32),
            pltpu.VMEM((n * packed, LANES), f32),
            pltpu.VMEM((8, root_total), f32),
            pltpu.VMEM((n - 1, 8, root_total), f32),
            pltpu.VMEM(view.shape, f32),
            pltpu.VMEM((2 * columns, 2 * root_total), jnp.bfloat16),
            pltpu.VMEM((2, chips) + chunk, f32),
            pltpu.VMEM((2, chips) + chunk, f32),
            pltpu.VMEM((2, chips) + chunk, f32),
            pltpu.VMEM((2, chips) + chunk, f32),
            pltpu.VMEM((outer_chips,) + chunk, f32),
            pltpu.VMEM((inner_chips,) + chunk, f32),
            pltpu.VMEM((outer_chips,) + chunk, f32),
            pltpu.VMEM((inner_chips,) + chunk, f32),
            dma((8,)),
            dma,
            dma,
            dma,
            dma,
            dma((2, chips)),
            dma((2, chips)),
            dma((2, chips)),
            dma((2, chips)),
            dma((outer_chips,)),
            dma((outer_chips,)),
            dma((inner_chips,)),
            dma((inner_chips,)),
        ],
        compiler_params=pltpu.CompilerParams(
            collective_id=0, has_side_effects=True, vmem_limit_bytes=60 * 1024 * 1024
        ),
    )(
        poles,
        coupling,
        payload,
        index,
        masked_z.reshape(-1, 1),
        masked_d.reshape(-1, 1),
        view,
    )
    merged = merged.reshape(rows, strips, 2, LANES).transpose(0, 2, 1, 3).reshape(rows, 2, root_total)
    return (position.reshape(root_total), merged)


def solution(mesh):
    in_specs = (
        P("groups", None, "row"),
        P(None, ("groups", "row")),
        P(None, ("groups", "row")),
        P(None, "groups"),
        P("groups"),
    )
    out_specs = (P("groups"), P(("groups", "row"), None, None))
    return jax.shard_map(body, mesh=mesh, in_specs=in_specs, out_specs=out_specs, check_vma=False)
```

time: 317 us -> 95.9 us (0.30)
  waiting for transfers between devices: 151 us -> 0 us
  blocking collectives: 117 us -> 0 us
  Pallas kernels: 0 us -> 86.8 us
  matrix products: 24.1 us -> 0 us
  between operations: 14.8 us -> 1.32 us
    reduce_scatter x1 -> x0, waiting for transfers between devices: 151 us -> none  [body(): lax.psum_scatter(jnp.einsum('isj,sjk->isk', sub_vectors, vectors, precisi...]
    pallas_call x0 -> x1, Pallas kernels: none -> 86.8 us  [body(): pl.pallas_call(functools.partial(kernel, n, inner_chips, packed, portion)...]
    all_gather x2 -> x0, blocking collectives: 80.2 us -> none  [the longest x1 43.4 us: body(): lax.all_gather(masked_z, 'row', axis=1, tiled=True)]
    unnamed x1 -> x0, blocking collectives: 37.1 us -> none
    dot_general x1 -> x0, matrix products: 24.1 us -> none  [body(): jnp.einsum('isj,sjk->isk', sub_vectors, vectors, precision=lax.Precision....]
  transfers between devices with their start and end apart: 1 -> 0, of which waited for: 1 -> 0; matrix products, arithmetic and copies ran while one was open for 0% -> 0% of each run, Pallas kernels for 0% -> 0%
where the time goes in v1:
time: 95.9 us; the launch traced here: 95.6 us
  Pallas kernels  86.8 us (91%)
  local copies, waits for them, and re-layouts  5.43 us (6%)
  other arithmetic  2.05 us (2%)
  between operations  1.32 us (1%)
    pallas_call x1, Pallas kernels, body(): pl.pallas_call(functools.partial(kernel, n, inner_chips, packed, portion)...  86.8 us
    unnamed x6, local copies, waits for them, and re-layouts  4.53 us

profile of v1, /device:TPU:0, one launch (start us, length us, event | category | flops | bytes accessed | tf_op | source)
XLA Modules:
  0.0 95.6 jit_solution(901611459419494218)
XLA Ops:
  1.3 0.1 add.30
  1.4 0.1 add.31
  1.5 0.1 broadcast_add_fusion
  1.5 0.7 slice_bitcast_fusion.1
  2.2 0.7 maximum_multiply_fusion
  3.0 0.6 pad_maximum_fusion.payload
  3.6 0.7 pad_add_fusion
  4.3 0.9 copy.12
  5.1 0.8 copy.14
  6.0 86.8 %shard_map.68 = (f32[1,128]{1,0:T(1,128)}, f32[512,128]{1,0:T(8,128)}) custom-call(s32[2,128]{1,0:T(2,128)} %poles.1, f32[1]{0:T(128)S(6)} %copy.17.coupling, f32[8,128]{1,0:T(8,128)} %pad_maximum_fusion.payload, s32[2,128,128]{2,1,0:T(8,128)} %bitcast.24, f32[512,1]{1,0:T(8,128)} %bitcast.22, f32[512,1]{1,0:T(8,128)} %bitcast.23, f32[32768,128]{1,0:T(8,128)} %bitcast.21), custom_call_target="tpu_custom_call" | custom-call | tf_op jit(solution)/shard_map/pallas_call | solution.py:324
  92.8 1.1 %copy.18 = f32[128]{0:T(128)} copy(f32[128]{0:T(128)} %bitcast.31) | data formatting | bytes 1024
  94.0 1.7 %copy.19 = f32[256,2,128]{2,1,0:T(2,128)} copy(f32[256,2,128]{2,1,0:T(2,128)} %bitcast.25) | data formatting | bytes 524288
  (9 shorter events, 0.1 us)

commit v2 on v1

v2 whole, which is shorter than its diff:
```python
import functools

import jax
import jax.numpy as jnp
from jax import lax
from jax.experimental import pallas as pl
from jax.experimental.pallas import tpu as pltpu
from jax.sharding import PartitionSpec as P

ITERS = 5
MESH = pl.DeviceIdType.MESH
LANES = 128


def total_of(x):
    return jnp.sum(jnp.sum(x, axis=0, keepdims=True), axis=1, keepdims=True)


def kernel(
    n,
    inner_chips,
    packed,
    portion,
    poles,
    coupling,
    payload,
    sub,
    position,
    merged,
    gathered,
    full_z,
    full_d,
    own_roots,
    roots,
    held,
    factors,
    partial,
    partner_partial,
    mine,
    arrived,
    reduced_a,
    reduced_b,
    last_a,
    last_b,
    load_sem,
    gather_send,
    gather_recv,
    roots_send,
    roots_recv,
    pair_send,
    pair_recv,
    first_send,
    first_recv,
    second_send,
    second_recv,
):
    me = lax.axis_index("row")
    chips = n // 2
    core = lax.rem(me, 2)
    chip = me // 2
    size_a = inner_chips
    size_b = chips // size_a
    place_a = lax.rem(chip, size_a)
    place_b = chip // size_a
    rows, root_total = partial.shape[2], partial.shape[3]
    tile_rows = sub.shape[0] // (rows * n)
    blocks = tile_rows // 2
    columns = blocks * LANES
    loads = load_sem.shape[0]
    load_rows = sub.shape[0] // loads

    def load(i):
        part = pl.ds(pl.multiple_of(i * load_rows, 8), load_rows)
        return pltpu.make_async_copy(sub.at[part], held.at[part], load_sem.at[i])

    for i in range(loads):
        load(i).start()

    barrier = pltpu.get_barrier_semaphore()

    def greet(i, carry):
        pl.semaphore_signal(barrier, inc=1, device_id={"row": lax.rem(me + i, n)}, device_id_type=MESH)
        return carry

    lax.fori_loop(1, n, greet, 0)
    pl.semaphore_wait(barrier, n - 1)

    def push(source, target, send, recv):
        def step(i, carry):
            pltpu.make_async_remote_copy(
                src_ref=source,
                dst_ref=target.at[i - 1],
                send_sem=send,
                recv_sem=recv,
                device_id={"row": lax.rem(me + i, n)},
                device_id_type=MESH,
            ).start()
            return carry

        lax.fori_loop(1, n, step, 0)

    def settle(target, sem):
        whole = target.at[pl.ds(0, n - 1)]
        pltpu.make_async_copy(whole, whole, sem).wait()

    push(payload, gathered, gather_send, gather_recv)
    padding = jnp.zeros((LANES - payload.shape[0], LANES), jnp.float32)
    standing = jnp.transpose(jnp.concatenate([payload[...], padding], axis=0))
    settle(gathered, gather_recv)
    half = payload.shape[0] // 2
    full_z[pl.ds(0, packed), :] = payload[pl.ds(0, packed), :]
    full_d[pl.ds(0, packed), :] = payload[pl.ds(half, packed), :]
    for i in range(1, n):
        full_z[pl.ds(i * packed, packed), :] = gathered[i - 1, pl.ds(0, packed), :]
        full_d[pl.ds(i * packed, packed), :] = gathered[i - 1, pl.ds(half, packed), :]
    values = full_d[...]
    weights = full_z[...] * full_z[...]
    line = lax.broadcasted_iota(jnp.int32, (n * packed, LANES), 0)
    slot = lax.shift_right_logical(line, jnp.full_like(line, packed.bit_length() - 1))
    line = line - slot * packed
    side = jnp.where(line >= blocks, 1, 0)
    owner = me - slot
    owner = jnp.where(owner < 0, owner + n, owner)
    order = rows * n
    places = side * order + owner * columns + (line - side * blocks) * LANES
    places = places + lax.broadcasted_iota(jnp.int32, (n * packed, LANES), 1)
    inverse_coupling = 1.0 / coupling[0]
    lane = lax.broadcasted_iota(jnp.int32, (1, root_total), 1)
    rows_out = [jnp.zeros((1, root_total), jnp.float32) for _ in range(4)]
    for r in range(portion):
        k = me * portion + r
        lower = total_of(jnp.where(places == poles[0, k], values, 0.0))
        spacing = total_of(jnp.where(places == poles[1, k], values, 0.0)) - lower
        shifted = values - lower
        offset = 0.5 * spacing
        for step in range(ITERS + 1):
            inverse = 1.0 / (shifted - offset)
            part = weights * inverse
            slope = total_of(part * inverse)
            if step < ITERS:
                moved = offset - (inverse_coupling + total_of(part)) / slope
                offset = jnp.minimum(jnp.maximum(moved, 0.02 * spacing), 0.98 * spacing)
        for i, value in enumerate((lower, spacing, offset, slope)):
            rows_out[i] = jnp.where(lane == k, value, rows_out[i])
    for i in range(4):
        own_roots[pl.ds(i, 1), :] = rows_out[i]
    own_roots[pl.ds(4, 4), :] = jnp.zeros((4, root_total), jnp.float32)
    push(own_roots, roots, roots_send, roots_recv)
    settle(roots, roots_recv)
    known = own_roots[...]
    for i in range(n - 1):
        known = known + roots[i]
    lower, spacing, offset, norm_sq = (known[i : i + 1, :] for i in range(4))
    position[...] = offset / spacing
    normalizer = 1.0 / jnp.sqrt(norm_sq)
    for i in range(packed):
        piece = pl.ds(i * LANES, LANES)
        z_column = standing[:, i : i + 1]
        d_column = standing[:, half + i : half + i + 1]
        vectors = z_column / ((d_column - lower) - offset) * normalizer
        top = vectors.astype(jnp.bfloat16)
        factors[piece, pl.ds(0, root_total)] = top
        factors[piece, pl.ds(root_total, root_total)] = (vectors - top.astype(jnp.float32)).astype(jnp.bfloat16)

    for i in range(loads):
        load(i).wait()

    crossing = rows * 7 // 16 // 8 * 8
    parts = ((0, 0, rows, 0), (1, 0, rows - crossing, 0), (1, rows - crossing, crossing, 1))
    outer = (size_b, size_a)
    inner = (size_a, size_b)

    def target_chip(kind, u, v):
        step_a, step_b = (v, u) if kind == 0 else (u, v)
        new_a = lax.rem(place_a + step_a + 1, size_a)
        new_b = lax.rem(place_b + step_b + 1, size_b)
        return new_a, new_b

    def product(p, t, which):
        s, first, count, kind = parts[p]
        new_a, new_b = target_chip(kind, t // inner[kind], lax.rem(t, inner[kind]))
        device = (new_b * size_a + new_a) * 2 + which
        start = device * (rows * tile_rows) + first * tile_rows
        pieces = [held[pl.ds(start + j * 2 + s, count, stride=tile_rows), :] for j in range(blocks)]
        a = pieces[0] if blocks == 1 else jnp.concatenate(pieces, axis=1)
        high = a.astype(jnp.bfloat16)
        low = (a - high.astype(jnp.float32)).astype(jnp.bfloat16)
        right = factors[pl.ds(s * columns, columns), :]
        both = jnp.dot(high, right, preferred_element_type=jnp.float32)
        small = jnp.dot(low, right[:, :root_total], preferred_element_type=jnp.float32)
        return both[:, :root_total] + (both[:, root_total:] + small)

    def block(ref, p, t):
        s, first, count, kind = parts[p]
        return ref.at[s, t, pl.ds(first, count)]

    def pair_copy(p, t):
        return pltpu.make_async_remote_copy(
            src_ref=block(partial, p, t),
            dst_ref=block(partner_partial, p, t),
            send_sem=pair_send.at[p, t],
            recv_sem=pair_recv.at[p, t],
            device_id={"row": chip * 2 + 1 - core},
            device_id_type=MESH,
        )

    def first_copy(p, t):
        kind = parts[p][3]
        new_a, new_b = target_chip(kind, t // inner[kind], lax.rem(t, inner[kind]))
        peer = place_b * size_a + new_a if kind == 0 else new_b * size_a + place_a
        return pltpu.make_async_remote_copy(
            src_ref=block(mine, p, t),
            dst_ref=block(arrived, p, t),
            send_sem=first_send.at[p, t],
            recv_sem=first_recv.at[p, t],
            device_id={"row": peer * 2 + core},
            device_id_type=MESH,
        )

    def leaves(p, t):
        kind = parts[p][3]
        return lax.rem(t, inner[kind]) != inner[kind] - 1

    count_parts = len(parts)

    def for_partner(t):
        for p in range(count_parts):
            block(partial, p, t)[...] = product(p, t, 1 - core)
            pair_copy(p, t).start()

    def for_self(t):
        for p in range(count_parts):
            value = product(p, t, core)
            pair_copy(p, t).wait_recv()
            block(mine, p, t)[...] = value + block(partner_partial, p, t)[...]

            @pl.when(leaves(p, t))
            def _():
                first_copy(p, t).start()

    lead = min(2, chips)
    for t in range(lead):
        for_partner(t)

    def both_ways(t, carry):
        for_self(t)
        for_partner(t + lead)
        return carry

    lax.fori_loop(0, chips - lead, both_ways, 0)

    def rest(t, carry):
        for_self(t)
        return carry

    lax.fori_loop(chips - lead, chips, rest, 0)

    def second_block(refs, p, u):
        s, first, count, kind = parts[p]
        return refs[kind].at[s, u, pl.ds(first, count)] if kind == 0 else refs[kind].at[u]

    reduced, last = (reduced_a, reduced_b), (last_a, last_b)

    def second_copy(p, u):
        kind = parts[p][3]
        new_a, new_b = target_chip(kind, u, u)
        peer = new_b * size_a + place_a if kind == 0 else place_b * size_a + new_a
        return pltpu.make_async_remote_copy(
            src_ref=second_block(reduced, p, u),
            dst_ref=second_block(last, p, u),
            send_sem=second_send.at[p, u],
            recv_sem=second_recv.at[p, u],
            device_id={"row": peer * 2 + core},
            device_id_type=MESH,
        )

    def fold(p, u):
        kind = parts[p][3]
        base = u * inner[kind]
        value = block(mine, p, base + inner[kind] - 1)[...]
        for v in range(inner[kind] - 1):
            first_copy(p, base + v).wait_recv()
            value = value + block(arrived, p, base + v)[...]
        second_block(reduced, p, u)[...] = value

    for u in range(max(outer)):
        for p in range(count_parts):
            size = outer[parts[p][3]]
            if u < size:
                fold(p, u)
                if u < size - 1:
                    second_copy(p, u).start()

    strips = root_total // LANES
    for p in range(count_parts):
        s, first, count, kind = parts[p]
        value = second_block(reduced, p, outer[kind] - 1)[...]
        for u in range(outer[kind] - 1):
            second_copy(p, u).wait_recv()
            value = value + second_block(last, p, u)[...]
        for strip in range(strips):
            target = pl.ds((first * strips + strip) * 2 + s, count, stride=2 * strips)
            merged[target, :] = value[:, strip * LANES : (strip + 1) * LANES]

    settle(gathered, gather_send)
    settle(roots, roots_send)

    def drain(t, carry):
        for p in range(count_parts):
            pair_copy(p, t).wait_send()

            @pl.when(leaves(p, t))
            def _():
                first_copy(p, t).wait_send()

        return carry

    lax.fori_loop(0, chips, drain, 0)
    for p in range(count_parts):
        for u in range(outer[parts[p][3]] - 1):
            second_copy(p, u).wait_send()


def body(sub_vectors, eigen_values, kept, poles, coupling):
    order, _, columns = sub_vectors.shape
    n = lax.axis_size("row")
    root_total = poles.shape[1]
    portion = root_total // n
    strips = root_total // LANES
    rows = order // n
    chips = n // 2
    inner_chips = 4 if chips % 4 == 0 else 1
    outer_chips = chips // inner_chips
    blocks = columns // LANES
    packed = 2 * blocks
    half = -(-packed // 4) * 4

    kept_float = kept.astype(jnp.float32)
    boundary = jnp.stack([sub_vectors[order - 1, 0, :], sub_vectors[0, 1, :]])
    masked_z = boundary * kept_float
    masked_d = eigen_values - 1000000.0 * (1.0 - kept_float)
    tall = lambda x: jnp.pad(x.reshape(packed, LANES), ((0, half - packed), (0, 0)))
    payload = jnp.concatenate([tall(masked_z), tall(masked_d)], axis=0)
    view = (
        sub_vectors.reshape(order, 2, blocks, LANES)
        .transpose(0, 2, 1, 3)
        .reshape(order * blocks * 2, LANES)
    )
    vmem = pl.BlockSpec(memory_space=pltpu.VMEM)
    smem = pl.BlockSpec(memory_space=pltpu.SMEM)
    chunk = (rows, root_total)
    crossing = rows * 7 // 16 // 8 * 8
    f32 = jnp.float32
    dma = pltpu.SemaphoreType.DMA
    position, merged = pl.pallas_call(
        functools.partial(kernel, n, inner_chips, packed, portion),
        out_shape=(
            jax.ShapeDtypeStruct((1, root_total), f32),
            jax.ShapeDtypeStruct((rows * 2 * strips, LANES), f32),
        ),
        in_specs=[smem, smem, vmem, pl.BlockSpec(memory_space=pl.ANY)],
        out_specs=(vmem, vmem),
        scratch_shapes=[
            pltpu.VMEM((n - 1, 2 * half, LANES), f32),
            pltpu.VMEM((n * packed, LANES), f32),
            pltpu.VMEM((n * packed, LANES), f32),
            pltpu.VMEM((8, root_total), f32),
            pltpu.VMEM((n - 1, 8, root_total), f32),
            pltpu.VMEM(view.shape, f32),
            pltpu.VMEM((2 * columns, 2 * root_total), jnp.bfloat16),
            pltpu.VMEM((2, chips) + chunk, f32),
            pltpu.VMEM((2, chips) + chunk, f32),
            pltpu.VMEM((2, chips) + chunk, f32),
            pltpu.VMEM((2, chips) + chunk, f32),
            pltpu.VMEM((2, outer_chips) + chunk, f32),
            pltpu.VMEM((inner_chips, crossing, root_total), f32),
            pltpu.VMEM((2, outer_chips) + chunk, f32),
            pltpu.VMEM((inner_chips, crossing, root_total), f32),
            dma((8,)),
            dma,
            dma,
            dma,
            dma,
            dma((3, chips)),
            dma((3, chips)),
            dma((3, chips)),
            dma((3, chips)),
            dma((3, max(inner_chips, outer_chips))),
            dma((3, max(inner_chips, outer_chips))),
        ],
        compiler_params=pltpu.CompilerParams(
            collective_id=0, has_side_effects=True, vmem_limit_bytes=60 * 1024 * 1024
        ),
    )(
        poles,
        coupling,
        payload,
        view,
    )
    merged = merged.reshape(rows, strips, 2, LANES).transpose(0, 2, 1, 3).reshape(rows, 2, root_total)
    return (position.reshape(root_total), merged)


def solution(mesh):
    in_specs = (
        P("groups", None, "row"),
        P(None, ("groups", "row")),
        P(None, ("groups", "row")),
        P(None, "groups"),
        P("groups"),
    )
    out_specs = (P("groups"), P(("groups", "row"), None, None))
    return jax.shard_map(body, mesh=mesh, in_specs=in_specs, out_specs=out_specs, check_vma=False)
```

time: 95.9 us -> 69.8 us (0.73)
  Pallas kernels: 86.8 us -> 63.3 us
  local copies, waits for them, and re-layouts: 5.43 us -> 3.59 us
    pallas_call x1, Pallas kernels: 86.8 us -> 63.3 us  [body(): pl.pallas_call(functools.partial(kernel, n, inner_chips, packed, portion)...]
    unnamed x6 -> x2, local copies, waits for them, and re-layouts: 4.53 us -> 2.86 us
where the time goes in v2:
time: 69.8 us; the launch traced here: 69.5 us
  Pallas kernels  63.3 us (91%)
  local copies, waits for them, and re-layouts  3.59 us (5%)
  other arithmetic  1.31 us (2%)
  between operations  1.29 us (2%)
    pallas_call x1, Pallas kernels, body(): pl.pallas_call(functools.partial(kernel, n, inner_chips, packed, portion)...  63.3 us
    unnamed x2, local copies, waits for them, and re-layouts  2.86 us

profile of v2, /device:TPU:0, one launch (start us, length us, event | category | flops | bytes accessed | tf_op | source)
XLA Modules:
  0.0 69.5 jit_solution(11356496103309481051)
XLA Ops:
  1.3 0.7 %slice_bitcast_fusion.1 = (f32[1,256]{1,0:T(1,128)S(1)}, f32[1,256]{1,0:T(1,128)S(1)}) fusion(f32[8192,2,256]{2,1,0:T(2,128)} %param.5), kind=kLoop, calls=%fused_computation.4 | loop fusion | bytes 4096 | tf_op jit(solution)/shard_map/stack;squeeze | solution.py:339
  2.0 0.7 %maximum_multiply_fusion = (f32[2,256]{1,0:T(2,128)S(1)}, f32[2,256]{1,0:T(2,128)S(1)}) fusion(f32[1,256]{1,0:T(1,128)S(1)} %get-tuple-element.7, f32[1,256]{1,0:T(1,128)S(1)} %get-tuple-element.6, s32[2,256]{1,0:T(2,128)} %param.7, f32[2,256]{1,0:T(2,128)} %param.6), kind=kLoop, calls=%fused_computation.1 | loop fusion | flops 3072 | bytes 10240 | tf_op jit(solution)/shard_map/mul | solution.py:340
  2.7 0.6 pad_maximum_fusion.payload
  3.3 63.3 %shard_map.68 = (f32[1,128]{1,0:T(1,128)}, f32[512,128]{1,0:T(8,128)}) custom-call(s32[2,128]{1,0:T(2,128)} %poles.1, f32[1]{0:T(128)S(6)} %copy.10.coupling, f32[8,128]{1,0:T(8,128)} %pad_maximum_fusion.payload, f32[32768,128]{1,0:T(8,128)} %bitcast.11), custom_call_target="tpu_custom_call" | custom-call | tf_op jit(solution)/shard_map/pallas_call | solution.py:355
  66.6 1.2 %copy.11 = f32[128]{0:T(128)} copy(f32[128]{0:T(128)} %bitcast.13) | data formatting | bytes 1024
  67.8 1.7 %copy.12 = f32[256,2,128]{2,1,0:T(2,128)} copy(f32[256,2,128]{2,1,0:T(2,128)} %bitcast.12) | data formatting | bytes 524288
  (2 shorter events, 0.0 us)
